TPU v7x, 16 devices: a 4x2x1 block of a 4x4x8 slice. The times are simulated.
16 devices in a mesh: rep: 2 (over y, z), dp: 8 (over x, core).
Axes of the slice: x: 4, y: 2, z: 1, core: 2. Of those that a mesh axis runs over, the one named last changes fastest.
The devices are a block of a 4x4x8 slice.
Arguments:
- x: bfloat16 [16, 2048, 768], P(('rep', 'dp')), parts along dimension 0
- dy: bfloat16 [16, 2048, 768], P(('rep', 'dp')), parts along dimension 0
- w_gate: bfloat16 [2, 768, 2304], replicated
- w_up: bfloat16 [2, 768, 2304], replicated
- w_down: bfloat16 [2, 2304, 768], replicated
- m_w_gate: float32 [2, 768, 2304], replicated
- m_w_up: float32 [2, 768, 2304], replicated
- m_w_down: float32 [2, 2304, 768], replicated
- v_w_gate: float32 [2, 768, 2304], replicated
- v_w_up: float32 [2, 768, 2304], replicated
- v_w_down: float32 [2, 2304, 768], replicated
Outputs:
- output 1: bfloat16 [4, 768, 2304], P('rep'), parts along dimension 0
- output 2: bfloat16 [4, 768, 2304], P('rep'), parts along dimension 0
- output 3: bfloat16 [4, 2304, 768], P('rep'), parts along dimension 0
- output 4: float32 [4, 768, 2304], P('rep'), parts along dimension 0
- output 5: float32 [4, 768, 2304], P('rep'), parts along dimension 0
- output 6: float32 [4, 2304, 768], P('rep'), parts along dimension 0
- output 7: float32 [4, 768, 2304], P('rep'), parts along dimension 0
- output 8: float32 [4, 768, 2304], P('rep'), parts along dimension 0
- output 9: float32 [4, 2304, 768], P('rep'), parts along dimension 0
There are 2 independent parts. A program takes and returns all parts, laid end to end along the dimension named above; an argument that names none is the same for every part.
All inputs are finite; a program needn't handle non-finite values.
Results may differ from a plain program's by a relative error of at most 0.022.
Values are sent between devices in bfloat16 or wider.
A program may use at most 768 MiB of HBM per device.

v0:
```python
import jax
import jax.numpy as jnp
from jax import lax
from jax.sharding import PartitionSpec as P

NAMES = ("w_gate", "w_up", "w_down")


def matmul(a, w):
    return jnp.dot(a, w, preferred_element_type=jnp.float32).astype(jnp.bfloat16)


def normed(h):
    wide = h.astype(jnp.float32)
    scale = lax.rsqrt(jnp.mean(wide**2, -1, keepdims=True) + 1e-6)
    return (wide * scale).astype(jnp.bfloat16)


def layer(h, w):
    a = normed(h)
    gate = jnp.dot(a, w["w_gate"], preferred_element_type=jnp.float32)
    up = jnp.dot(a, w["w_up"], preferred_element_type=jnp.float32)
    return h + matmul((jax.nn.silu(gate) * up).astype(jnp.bfloat16), w["w_down"])


def adamw(w, m, v, g):
    m = 0.9 * m + 0.1 * g
    v = 0.95 * v + 0.05 * g * g
    step = m * lax.rsqrt(v + 1e-8) + 0.1 * w
    return (w - 0.02 * step).astype(jnp.bfloat16), m, v


def solution(mesh):
    def step(x, dy, *arrays):
        weights, m, v = (arrays[i : i + 3] for i in (0, 3, 6))
        layers = weights[0].shape[0]
        h, kept = x[0], []
        for number in range(layers):
            kept.append(h)
            h = layer(h, {name: w[number] for name, w in zip(NAMES, weights, strict=True)})
        by_h, summed = dy[0], [None] * layers
        for number in reversed(range(layers)):
            _, back = jax.vjp(lambda w, h: layer(h, w), {name: w[number] for name, w in zip(NAMES, weights, strict=True)}, kept[number])
            by_w, by_h = back(by_h)
            summed[number] = [lax.psum(by_w[name], "dp") for name in NAMES]
        gradients = [jnp.stack([summed[number][i] for number in range(layers)]).astype(jnp.float32) for i in range(3)]
        new = [adamw(w.astype(jnp.float32), m, v, g) for w, m, v, g in zip(weights, m, v, gradients, strict=True)]
        return tuple(one[which] for which in range(3) for one in new)

    return jax.shard_map(
        step,
        mesh=mesh,
        in_specs=(P(("rep", "dp"), None, None),) * 2 + (P(None, None, None),) * 9,
        out_specs=(P("rep", None, None),) * 9,
        check_vma=False,
    )
```

profile of v0, /device:TPU:112, one launch (start us, length us, event | category | flops | bytes accessed | tf_op | source)
XLA Modules:
  0.0 555.1 jit_solution(7091195044939739656)
XLA Ops:
  7.2 0.1 all-reduce.3.cloned.1.call-start
  7.3 3.2 copy.20
  10.5 0.0 copy-start
  10.5 0.7 fusion.30
  11.2 5.0 copy.21
  16.2 12.5 %convolution_convert_fusion.1 = bf16[2048,2304]{1,0:T(8,128)(2,1)} fusion(bf16[2,2304,768]{2,1,0:T(8,128)(2,1)} %param.15, bf16[1,2048,768]{2,1,0:T(8,128)(2,1)} %param.12), kind=kOutput, calls=%fused_computation.50 | convolution fusion | flops 7252475904 | bytes 16121856 | tf_op jit(solution)/shard_map/transpose(jvp())/dot_general | solution.py:10
  28.7 0.0 copy-done.4
  28.7 13.0 %fusion.64 = f32[2048,2304]{1,0:T(8,128)} fusion(bf16[2,768,2304]{2,1,0:T(8,128)(2,1)} %param.13, bf16[1,2048,768]{2,1,0:T(8,128)(2,1)S(1)} %copy-done.4, f32[2048]{0:T(1024)S(1)} %add_rsqrt_fusion), kind=kOutput, calls=%fused_computation.96 | convolution fusion | flops 7252475904 | bytes 25567232 | tf_op jit(solution)/shard_map/dot_general | solution.py:21
  41.7 0.0 copy-done.10
  41.7 19.0 %multiply_convert_fusion.1 = (bf16[2048,2304]{1,0:T(8,128)(2,1)}, f32[2048,2304]{1,0:T(8,128)}) fusion(f32[2048,2304]{1,0:T(8,128)} %fusion.64, bf16[2,768,2304]{2,1,0:T(8,128)(2,1)} %param.14, bf16[1,2048,768]{2,1,0:T(8,128)(2,1)} %param.11, f32[2048]{0:T(1024)S(1)} %add_rsqrt_fusion), kind=kOutput, calls=%fused_computation.20 | convolution fusion | flops 7280787456 | bytes 53878784 | tf_op jit(solution)/shard_map/dot_general | solution.py:22
  60.7 0.0 copy-done
  60.7 11.9 %fusion.34 = (f32[2048]{0:T(1024)S(1)}, bf16[2048,768]{0,1:T(8,128)(2,1)S(1)}) fusion(bf16[2048,2304]{1,0:T(8,128)(2,1)} %get-tuple-element.24, bf16[2,2304,768]{2,1,0:T(8,128)(2,1)} %param.15, bf16[1,2048,768]{1,2,0:T(8,128)(2,1)S(1)} %copy.20), kind=kOutput, calls=%fused_computation.67 | convolution fusion | flops 7255619584 | bytes 19275776 | tf_op jit(solution)/shard_map/dot_general | solution.py:10
  72.6 0.0 copy-start.8
  72.6 0.0 copy-start.6
  72.6 0.6 copy-done.8
  73.2 1.1 copy-done.6
  74.3 13.5 %fusion.51 = f32[2048,2304]{1,0:T(8,128)} fusion(bf16[2,768,2304]{2,1,0:T(8,128)(2,1)} %param.14, bf16[2048,768]{0,1:T(8,128)(2,1)S(1)} %get-tuple-element.27, f32[2048]{0:T(1024)S(1)} %fusion.102), kind=kOutput, calls=%fused_computation.83 | convolution fusion | flops 7252475904 | bytes 25567232 | tf_op jit(solution)/shard_map/jvp()/dot_general | solution.py:22
  87.8 30.8 %fusion.2 = (bf16[2048,2304]{1,0:T(8,128)(2,1)}, f32[2048,2304]{1,0:T(8,128)}) fusion(f32[2048,2304]{1,0:T(8,128)} %fusion.51, bf16[2048,2304]{1,0:T(8,128)(2,1)} %convolution_convert_fusion.1, bf16[2,768,2304]{2,1,0:T(8,128)(2,1)} %param.13, bf16[2048,768]{0,1:T(8,128)(2,1)} %copy-done.6, f32[2048]{0:T(1024)S(1)} %fusion.102), kind=kOutput, calls=%fused_computation.11 | convolution fusion | flops 7309099008 | bytes 63315968 | tf_op jit(solution)/shard_map/jvp()/dot_general | solution.py:21
  118.6 0.0 slice-done.2
  118.6 0.0 slice-done.3
  118.6 0.0 copy-start.7
  118.6 0.0 copy-start.12
  118.6 11.3 %fusion.72 = bf16[2048,768]{0,1:T(8,128)(2,1)} fusion(bf16[2048,2304]{1,0:T(8,128)(2,1)} %get-tuple-element.28, bf16[2,768,2304]{2,1,0:T(8,128)(2,1)S(1)} %bitcast.83), kind=kOutput, calls=%fused_computation.102 | convolution fusion | flops 7247757312 | bytes 16121856 | tf_op jit(solution)/shard_map/transpose(jvp())/dot_general | solution.py:21
  130.0 0.0 copy-done.7
  130.0 0.0 copy-done.12
  130.0 8.9 %fusion.44 = bf16[1,768,2304]{2,1,0:T(8,128)(2,1)} fusion(bf16[2048,2304]{1,0:T(8,128)(2,1)S(1)} %copy-done.12, bf16[2048,768]{0,1:T(8,128)(2,1)S(1)} %copy-done.7, f32[2048]{0:T(1024)S(1)} %fusion.102), kind=kOutput, calls=%fused_computation.78 | convolution fusion | flops 7252475904 | bytes 16130048 | tf_op jit(solution)/shard_map/transpose(jvp())/dot_general | solution.py:21
  138.9 0.0 copy-done.5
  138.9 17.8 %fusion.43 = bf16[1,2304,768]{2,1,0:T(8,128)(2,1)} fusion(f32[2048,2304]{1,0:T(8,128)} %fusion.51, bf16[1,2048,768]{2,1,0:T(8,128)(2,1)S(1)} %copy-done.5, f32[2048,2304]{1,0:T(8,128)} %get-tuple-element.29), kind=kOutput, calls=%fused_computation.77 | convolution fusion | flops 7277838336 | bytes 44433408 | tf_op jit(solution)/shard_map/transpose(jvp())/dot_general | solution.py:10
  156.7 16.4 %fusion.50 = bf16[1,768,2304]{2,1,0:T(8,128)(2,1)} fusion(bf16[2048,2304]{1,0:T(8,128)(2,1)} %convolution_convert_fusion.1, bf16[2048,768]{0,1:T(8,128)(2,1)} %copy-done.6, f32[2048]{0:T(1024)S(1)} %fusion.102, f32[2048,2304]{1,0:T(8,128)} %get-tuple-element.29), kind=kOutput, calls=%fused_computation.82 | convolution fusion | flops 7282556928 | bytes 35004416 | tf_op jit(solution)/shard_map/transpose(jvp())/dot_general | solution.py:22
  173.1 19.6 %fusion.36 = (f32[2048]{0:T(1024)S(1)}, bf16[2048,768]{0,1:T(8,128)(2,1)}) fusion(bf16[2048,768]{0,1:T(8,128)(2,1)} %copy-done.6, bf16[2048,768]{0,1:T(8,128)(2,1)} %fusion.72, bf16[2,768,2304]{2,1,0:T(8,128)(2,1)} %param.14, bf16[2048,2304]{1,0:T(8,128)(2,1)} %convolution_convert_fusion.1, f32[2048,2304]{1,0:T(8,128)} %get-tuple-element.29), kind=kOutput, calls=%fused_computation.69 | convolution fusion | flops 7285504000 | bytes 41295872 | tf_op jit(solution)/shard_map/transpose(jvp())/dot_general | solution.py:22
  192.7 0.0 copy-done.9
  192.8 0.0 copy-done.2
  192.8 0.0 slice-start
  192.8 5.2 fusion.80
  198.0 0.0 slice-start.1
  198.0 11.6 %fusion.45 = bf16[1,2304,768]{2,1,0:T(8,128)(2,1)} fusion(bf16[2048,2304]{1,0:T(8,128)(2,1)} %get-tuple-element.24, bf16[2048,768]{0,1:T(8,128)(2,1)S(1)} %fusion.80), kind=kOutput, calls=%fused_computation.79 | convolution fusion | flops 7249526784 | bytes 16121856 | tf_op jit(solution)/shard_map/transpose(jvp())/dot_general | solution.py:10
  209.6 0.0 slice-done
  209.6 0.0 slice-done.1
  209.6 0.0 copy-start.11
  209.6 10.3 %convolution_convert_fusion = bf16[2048,2304]{1,0:T(8,128)(2,1)} fusion(bf16[2048,768]{0,1:T(8,128)(2,1)S(1)} %fusion.80, bf16[2,2304,768]{2,1,0:T(8,128)(2,1)S(1)} %bitcast.81), kind=kOutput, calls=%fused_computation.49 | convolution fusion | flops 7252475904 | bytes 16121856 | tf_op jit(solution)/shard_map/transpose(jvp())/dot_general | solution.py:10
  219.9 0.0 copy-done.11
  219.9 15.6 %fusion.46 = bf16[1,768,2304]{2,1,0:T(8,128)(2,1)} fusion(bf16[2048,2304]{1,0:T(8,128)(2,1)} %convolution_convert_fusion, f32[2048,2304]{1,0:T(8,128)} %fusion.64, bf16[1,2048,768]{1,2,0:T(8,128)(2,1)S(1)} %copy-done.1, f32[2048]{0:T(1024)S(1)} %copy-done.11), kind=kOutput, calls=%fused_computation.80 | convolution fusion | flops 7282556928 | bytes 35004416 | tf_op jit(solution)/shard_map/transpose(jvp())/dot_general | solution.py:22
  235.5 20.2 %fusion.47 = bf16[1,768,2304]{2,1,0:T(8,128)(2,1)} fusion(f32[2048,2304]{1,0:T(8,128)} %fusion.64, f32[2048,2304]{1,0:T(8,128)} %get-tuple-element.25, bf16[2048,2304]{1,0:T(8,128)(2,1)} %convolution_convert_fusion, bf16[1,2048,768]{1,2,0:T(8,128)(2,1)S(1)} %copy-done.1, f32[2048]{0:T(1024)S(1)} %copy-done.11), kind=kOutput, calls=%fused_computation.81 | convolution fusion | flops 7306149888 | bytes 53878784 | tf_op jit(solution)/shard_map/transpose(jvp())/dot_general | solution.py:21
  255.7 0.1 all-reduce.3.cloned.1.call-update
  255.7 219.5 %all-reduce.3.cloned.1.call-done = (bf16[1,768,2304]{2,1,0:T(8,128)(2,1)}, bf16[1,768,2304]{2,1,0:T(8,128)(2,1)}, bf16[1,768,2304]{2,1,0:T(8,128)(2,1)}, bf16[1,...) async-done(((bf16[1,768,2304]{2,1,0:T(8,128)(2,1)}, bf16[1,768,2304]{2,1,0:T(8,128)(2,1)}, bf16[1,768,2304]{2,1,0:T(8,128)(2,1)}, ...) | async-done | bytes 21233680 | tf_op jit(solution)/shard_map/psum | solution.py:45
  475.2 25.0 %fusion.21 = (bf16[2,2304,768]{2,1,0:T(8,128)(2,1)}, f32[2,2304,768]{2,1,0:T(8,128)}, f32[2,2304,768]{2,1,0:T(8,128)}) fusion(bf16[2,2304,768]{2,1,0:T(8,128)(2,1)} %param.15, bf16[1,2304,768]{2,1,0:T(8,128)(2,1)} %get-tuple-element.13, bf16[1,2304,768]{2,1,0:T(8,128)(2,1)} %get-tuple-element.14, f32[2,2304,768]{2,1,0:T(8,128)} %param.21, ...), kind=kLoop, calls=%fused_computation.42 | loop fusion | flops 67239936 | bytes 77856768 | tf_op jit(solution)/shard_map/convert_element_type | solution.py:30
  500.2 0.0 copy-done.3
  500.2 47.4 %fusion.13 = (bf16[2,768,2304]{2,1,0:T(8,128)(2,1)}, f32[2,768,2304]{2,1,0:T(8,128)}, f32[2,768,2304]{2,1,0:T(8,128)}, bf16[2,768,2304]{2,1,0:T(8,128)(2,1)}, f3...) fusion(bf16[2,768,2304]{2,1,0:T(8,128)(2,1)} %param.13, bf16[1,768,2304]{2,1,0:T(8,128)(2,1)S(1)} %copy-done.3, ...), kind=kLoop, calls=%fused_computation.34 | loop fusion | flops 134479872 | bytes 155713536 | tf_op jit(solution)/shard_map/convert_element_type | solution.py:30
  (15 shorter events, 0.0 us)
Async XLA Ops:
  7.2 468.1 %all-reduce.3.cloned.1.call-start = ((), (), s32[]{:S(2)}) async-start(), calls=%async_computation | async-start | bytes 42467328 | tf_op jit(solution)/shard_map/psum | solution.py:45
  10.5 50.2 %copy-start = (bf16[1,2048,768]{1,2,0:T(8,128)(2,1)}, bf16[1,2048,768]{1,2,0:T(8,128)(2,1)S(1)}, u32[]{:S(2)}) copy-start(bf16[1,2048,768]{1,2,0:T(8,128)(2,1)S(1)} %copy.20) | copy-start | bytes 9437188
  11.1 30.6 %copy-start.10 = (f32[2048]{0:T(1024)}, f32[2048]{0:T(1024)S(1)}, u32[]{:S(2)}) copy-start(f32[2048]{0:T(1024)S(1)} %add_rsqrt_fusion) | copy-start | bytes 24580
  16.2 12.6 %copy-start.4 = (bf16[1,2048,768]{2,1,0:T(8,128)(2,1)S(1)}, bf16[1,2048,768]{2,1,0:T(8,128)(2,1)}, u32[]{:S(2)}) copy-start(bf16[1,2048,768]{2,1,0:T(8,128)(2,1)} %param.11) | copy-start | bytes 9437188
  72.6 0.6 copy-start.8
  72.6 1.7 copy-start.6
  74.3 44.3 %slice-start.2 = ((s8[7077888]{0:T(1024)(128)(4,1)}), s8[4194304]{0:T(1024)(128)(4,1)S(1)}, s32[]{:S(2)}) async-start(s8[7077888]{0:T(1024)(128)(4,1)} %bitcast.82), calls=%async_computation.3 | async-start | bytes 8388608
  87.8 30.8 %slice-start.3 = ((s8[7077888]{0:T(1024)(128)(4,1)}), s8[2883584]{0:T(1024)(128)(4,1)S(1)}, s32[]{:S(2)}) async-start(s8[7077888]{0:T(1024)(128)(4,1)} %bitcast.82), calls=%async_computation.4 | async-start | bytes 5767168
  118.6 11.4 %copy-start.7 = (bf16[2048,768]{0,1:T(8,128)(2,1)S(1)}, bf16[2048,768]{0,1:T(8,128)(2,1)}, u32[]{:S(2)}) copy-start(bf16[2048,768]{0,1:T(8,128)(2,1)} %copy-done.6) | copy-start | bytes 9437188
  118.6 11.3 %copy-start.12 = (bf16[2048,2304]{1,0:T(8,128)(2,1)S(1)}, bf16[2048,2304]{1,0:T(8,128)(2,1)}, u32[]{:S(2)}) copy-start(bf16[2048,2304]{1,0:T(8,128)(2,1)} %get-tuple-element.28) | copy-start | bytes 28311556
  130.0 8.9 %copy-start.5 = (bf16[1,2048,768]{2,1,0:T(8,128)(2,1)S(1)}, bf16[1,2048,768]{2,1,0:T(8,128)(2,1)}, u32[]{:S(2)}) copy-start(bf16[1,2048,768]{2,1,0:T(8,128)(2,1)} %param.12) | copy-start | bytes 9437188
  173.1 19.6 %copy-start.9 = (f32[2048]{0:T(1024)S(1)}, f32[2048]{0:T(1024)}, u32[]{:S(2)}) copy-start(f32[2048]{0:T(1024)} %copy-done.8) | copy-start | bytes 24580
  173.1 19.6 %copy-start.2 = (bf16[1,2048,768]{1,2,0:T(8,128)(2,1)S(1)}, bf16[1,2048,768]{1,2,0:T(8,128)(2,1)}, u32[]{:S(2)}) copy-start(bf16[1,2048,768]{1,2,0:T(8,128)(2,1)} %copy.21) | copy-start | bytes 9437188
  192.8 16.8 %slice-start = ((s8[7077888]{0:T(1024)(128)(4,1)}), s8[4194304]{0:T(1024)(128)(4,1)S(1)}, s32[]{:S(2)}) async-start(s8[7077888]{0:T(1024)(128)(4,1)} %bitcast.80), calls=%async_computation.1 | async-start | bytes 8388608
  198.0 11.6 %slice-start.1 = ((s8[7077888]{0:T(1024)(128)(4,1)}), s8[2883584]{0:T(1024)(128)(4,1)S(1)}, s32[]{:S(2)}) async-start(s8[7077888]{0:T(1024)(128)(4,1)} %bitcast.80), calls=%async_computation.2 | async-start | bytes 5767168
  209.6 10.3 %copy-start.1 = (bf16[1,2048,768]{1,2,0:T(8,128)(2,1)S(1)}, bf16[1,2048,768]{1,2,0:T(8,128)(2,1)}, u32[]{:S(2)}) copy-start(bf16[1,2048,768]{1,2,0:T(8,128)(2,1)} %copy-done) | copy-start | bytes 9437188
  209.6 10.3 %copy-start.11 = (f32[2048]{0:T(1024)S(1)}, f32[2048]{0:T(1024)}, u32[]{:S(2)}) copy-start(f32[2048]{0:T(1024)} %copy-done.10) | copy-start | bytes 24580
  475.2 25.0 %copy-start.3 = (bf16[1,768,2304]{2,1,0:T(8,128)(2,1)S(1)}, bf16[1,768,2304]{2,1,0:T(8,128)(2,1)}, u32[]{:S(2)}) copy-start(bf16[1,768,2304]{2,1,0:T(8,128)(2,1)} %get-tuple-element.9) | copy-start | bytes 10616836
Sparse Core Ops, SparseCore 0:
  255.8 219.3 all-reduce.2
where the time goes:
time: 563 us; the launch traced here: 555 us
  matrix products  232 us (41%)
  waiting for transfers between devices  220 us (39%)
  other arithmetic  78.3 us (14%)
  between operations  14.7 us (3%)
  local copies, waits for them, and re-layouts  9.94 us (2%)
    psum x1, waiting for transfers between devices, step(): summed[number] = [lax.psum(by_w[name], 'dp') for name in NAMES]  220 us
    dot_general x5, matrix products, layer(): gate = jnp.dot(a, w['w_gate'], preferred_element_type=jnp.float32)  84.2 us
    dot_general x5, matrix products, layer(): up = jnp.dot(a, w['w_up'], preferred_element_type=jnp.float32)  84.1 us
    convert_element_type x2, other arithmetic, adamw(): return ((w - 0.02 * step).astype(jnp.bfloat16), m, v)  72.4 us
    dot_general x5, matrix products, matmul(): jnp.dot(a, w, preferred_element_type=jnp.float32).astype(jnp.bfloat16)  64.1 us
  transfers between devices with their start and end apart: 1, of which 1 were waited for; matrix products, arithmetic and copies ran while one was open for 0% of the time, Pallas kernels for 0%

commit v1 on v0

v1 whole, which is shorter than its diff:
```python
import functools

import jax
import jax.numpy as jnp
from jax import lax
from jax.experimental import pallas as pl
from jax.experimental.pallas import tpu as pltpu
from jax.sharding import PartitionSpec as P

BF16, F32 = jnp.bfloat16, jnp.float32
FB = 256
FB_FWD = 768
TT = 512
VMEM = 60 * 2**20


def dot(a, b):
    return jnp.dot(a, b, preferred_element_type=F32)


def dot_nt(a, b):
    return lax.dot_general(a, b, (((1,), (1,)), ((), ())), preferred_element_type=F32)


def transposed(eye, x):
    return dot_nt(eye, x).astype(BF16)


def scale_of(wide):
    return lax.rsqrt(jnp.mean(wide * wide, -1, keepdims=True) + 1e-6)


def sigmoid(x):
    return 1.0 / (1.0 + jnp.exp(-x))


def forward_kernel(h_ref, wg_ref, wu_ref, wd_ref, out_ref, a_ref, acc_ref):
    step, steps = pl.program_id(0), pl.num_programs(0)
    tokens = h_ref.shape[0]

    @pl.when(step == 0)
    def _():
        def tile(i, _):
            rows = pl.ds(i * TT, TT)
            wide = h_ref[rows, :].astype(F32)
            a_ref[rows, :] = (wide * scale_of(wide)).astype(BF16)
            acc_ref[rows, :] = jnp.zeros((TT, acc_ref.shape[1]), F32)
            return 0

        lax.fori_loop(0, tokens // TT, tile, 0)

    def tile(i, _):
        rows = pl.ds(i * TT, TT)
        a = a_ref[rows, :]
        gate = dot(a, wg_ref[0])
        up = dot(a, wu_ref[0])
        hid = (gate * sigmoid(gate) * up).astype(BF16)
        acc_ref[rows, :] += dot(hid, wd_ref[0])
        return 0

    lax.fori_loop(0, tokens // TT, tile, 0)

    @pl.when(step == steps - 1)
    def _():
        def tile(i, _):
            rows = pl.ds(i * TT, TT)
            down = acc_ref[rows, :].astype(BF16).astype(F32)
            out_ref[rows, :] = (h_ref[rows, :].astype(F32) + down).astype(BF16)
            return 0

        lax.fori_loop(0, tokens // TT, tile, 0)


def forward(h, weights, number):
    tokens, d = h.shape
    ff = weights[0].shape[2]
    return pl.pallas_call(
        forward_kernel,
        grid=(ff // FB_FWD,),
        in_specs=[
            pl.BlockSpec((tokens, d), lambda f: (0, 0), pipeline_mode=pl.Buffered(1)),
            pl.BlockSpec((1, d, FB_FWD), lambda f: (number, 0, f)),
            pl.BlockSpec((1, d, FB_FWD), lambda f: (number, 0, f)),
            pl.BlockSpec((1, FB_FWD, d), lambda f: (number, f, 0)),
        ],
        out_specs=pl.BlockSpec((tokens, d), lambda f: (0, 0), pipeline_mode=pl.Buffered(1)),
        out_shape=jax.ShapeDtypeStruct((tokens, d), BF16),
        scratch_shapes=[pltpu.VMEM((tokens, d), BF16), pltpu.VMEM((tokens, d), F32)],
        compiler_params=pltpu.CompilerParams(vmem_limit_bytes=VMEM, dimension_semantics=("arbitrary",)),
        cost_estimate=pl.CostEstimate(flops=6 * tokens * d * ff, bytes_accessed=4 * tokens * d + 6 * d * ff, transcendentals=tokens * ff),
        name="layer_forward",
    )(h, *weights)


SLOTS = 4
MESH = pl.DeviceIdType.MESH


def backward_kernel(with_input, n, h_ref, g_ref, wg_ref, wu_ref, wd_ref, *refs):
    if with_input:
        shard_ref, dh_ref, *refs, acc_ref = refs
    else:
        shard_ref, *refs = refs
    a_ref, at_ref, gt_ref, hid_ref, dgate_ref, dup_ref, own, recv_a, send_b, recv_b, send_c, recv_c, *sems = refs
    send_a_sem, recv_a_sem, send_b_sem, recv_b_sem, send_c_sem, recv_c_sem = sems
    step, blocks = pl.program_id(0), pl.num_programs(0) - SLOTS
    tokens, d = h_ref.shape
    share, half = own.shape[3], own.shape[3] // 2
    chips = n // 2
    me = lax.axis_index("dp")
    chip, core = lax.div(me, 2), lax.rem(me, 2)
    right_chip, far_chip, left_chip = (lax.rem(chip + i, chips) for i in (1, 2, 3))
    partner = chip * 2 + (1 - core)
    sides = (right_chip * 2 + core, left_chip * 2 + core)

    def copy_a(block):
        slot = lax.rem(block, SLOTS)
        return pltpu.make_async_remote_copy(
            own.at[slot, 1 - core], recv_a.at[slot], send_a_sem.at[slot], recv_a_sem.at[slot], device_id={"dp": partner}, device_id_type=MESH
        )

    def copy_b(block, way):
        slot = lax.rem(block, SLOTS)
        return pltpu.make_async_remote_copy(
            send_b.at[slot, way],
            recv_b.at[slot, way],
            send_b_sem.at[slot, way],
            recv_b_sem.at[slot, way],
            device_id={"dp": sides[way]},
            device_id_type=MESH,
        )

    def copy_c(block, way):
        slot = lax.rem(block, SLOTS)
        return pltpu.make_async_remote_copy(
            send_c.at[slot, way],
            recv_c.at[slot, way],
            send_c_sem.at[slot, way],
            recv_c_sem.at[slot, way],
            device_id={"dp": sides[way]},
            device_id_type=MESH,
        )

    def on_chip(slot, which, rows):
        return own[slot, core, which, rows].astype(F32) + recv_a[slot, which, rows].astype(F32)

    @pl.when(step == 0)
    def _():
        barrier = pltpu.get_barrier_semaphore()
        for other in (partner, *sides):
            pl.semaphore_signal(barrier, inc=1, device_id={"dp": other}, device_id_type=MESH)

    @pl.when(step == 1)
    def _():
        pl.semaphore_wait(pltpu.get_barrier_semaphore(), 3)

    first, second = pl.ds(0, half), pl.ds(half, half)

    @pl.when(step >= 4)
    def _():
        block = step - 4
        slot = lax.rem(block, SLOTS)
        copy_c(block, 0).wait()
        copy_c(block, 1).wait()
        for rows in (first, second):
            total = on_chip(slot, chip, rows) + recv_c[slot, 0, rows].astype(F32) + recv_c[slot, 1, rows].astype(F32)
            shard_ref[0, rows] = total.astype(BF16)

    @pl.when((step >= 3) & (step < blocks + 3))
    def _():
        block = step - 3
        slot = lax.rem(block, SLOTS)
        copy_b(block, 0).wait()
        copy_b(block, 1).wait()
        send_c[slot, 0, first] = (on_chip(slot, right_chip, first) + recv_b[slot, 0].astype(F32)).astype(BF16)
        send_c[slot, 0, second] = on_chip(slot, right_chip, second).astype(BF16)
        send_c[slot, 1, first] = on_chip(slot, left_chip, first).astype(BF16)
        send_c[slot, 1, second] = (on_chip(slot, left_chip, second) + recv_b[slot, 1].astype(F32)).astype(BF16)
        copy_c(block, 0).start()
        copy_c(block, 1).start()

    @pl.when((step >= 2) & (step < blocks + 2))
    def _():
        block = step - 2
        slot = lax.rem(block, SLOTS)
        copy_a(block).wait()
        send_b[slot, 0] = on_chip(slot, far_chip, first).astype(BF16)
        send_b[slot, 1] = on_chip(slot, far_chip, second).astype(BF16)
        copy_b(block, 0).start()
        copy_b(block, 1).start()

    @pl.when((step >= 1) & (step < blocks + 1))
    def _():
        copy_a(step - 1).start()

    eye = (lax.broadcasted_iota(jnp.int32, (FB, FB), 0) == lax.broadcasted_iota(jnp.int32, (FB, FB), 1)).astype(BF16)

    @pl.when(step == 0)
    def _():
        def tile(i, _):
            rows = pl.ds(pl.multiple_of(i * TT, TT), TT)
            wide = h_ref[rows, :].astype(F32)
            a_ref[rows, :] = (wide * scale_of(wide)).astype(BF16)
            for j in range(d // FB):
                at_ref[j * FB : (j + 1) * FB, rows] = transposed(eye, a_ref[rows, j * FB : (j + 1) * FB])
                gt_ref[j * FB : (j + 1) * FB, rows] = transposed(eye, g_ref[rows, j * FB : (j + 1) * FB])
            if with_input:
                acc_ref[rows, :] = jnp.zeros((TT, d), F32)
            return 0

        lax.fori_loop(0, tokens // TT, tile, 0)

    @pl.when(step < blocks)
    def _():
        slot = lax.rem(step, SLOTS)
        wg, wu, wd = wg_ref[0], wu_ref[0], wd_ref[0]
        for i in range(tokens // TT):
            rows = pl.ds(i * TT, TT)
            a = a_ref[rows, :]
            gate, up = dot(a, wg), dot(a, wu)
            dhid = dot_nt(g_ref[rows, :], wd).astype(BF16).astype(F32)
            sig = sigmoid(gate)
            silu = gate * sig
            hid_ref[rows, :] = (silu * up).astype(BF16)
            dup_ref[rows, :] = (dhid * silu).astype(BF16)
            dgate_ref[rows, :] = (dhid * up * (sig + silu * (1.0 - sig))).astype(BF16)
        part, down = d // n, FB // n
        for i in range(d // FB):
            rows = pl.ds(i * FB, FB)
            dwg = dot(at_ref[rows, :], dgate_ref[...]).astype(BF16)
            dwu = dot(at_ref[rows, :], dup_ref[...]).astype(BF16)
            dwd = transposed(eye, dot(gt_ref[rows, :], hid_ref[...]).astype(BF16))
            lo, hi = i * FB, (i + 1) * FB
            for k in range(n):
                top, end = max(lo, k * part), min(hi, (k + 1) * part)
                if top < end:
                    own[slot, k % 2, k // 2, top - k * part : end - k * part, :] = dwg[top - lo : end - lo]
                    own[slot, k % 2, k // 2, part + top - k * part : part + end - k * part, :] = dwu[top - lo : end - lo]
                own[slot, k % 2, k // 2, 2 * part + i * down : 2 * part + (i + 1) * down, :] = dwd[k * down : (k + 1) * down]
        if with_input:
            for i in range(tokens // TT):
                rows = pl.ds(i * TT, TT)
                acc_ref[rows, :] += dot_nt(dgate_ref[rows, :], wg) + dot_nt(dup_ref[rows, :], wu)

    if with_input:

        @pl.when(step == blocks)
        def _():
            def tile(i, _):
                rows = pl.ds(i * TT, TT)
                wide = h_ref[rows, :].astype(F32)
                scale = scale_of(wide)
                da = acc_ref[rows, :].astype(BF16).astype(F32)
                along = jnp.mean(da * wide, -1, keepdims=True)
                dwide = (da * scale - wide * (scale * scale * scale * along)).astype(BF16)
                dh_ref[rows, :] = (g_ref[rows, :].astype(F32) + dwide.astype(F32)).astype(BF16)
                return 0

            lax.fori_loop(0, tokens // TT, tile, 0)


def backward(h, g, weights, number, n, with_input):
    tokens, d = h.shape
    ff = weights[0].shape[2]
    blocks = ff // FB
    chips, share = n // 2, 3 * d // n
    assert chips == 4
    whole = pl.BlockSpec((tokens, d), lambda f: (0, 0), pipeline_mode=pl.Buffered(1))
    outs = [jax.ShapeDtypeStruct((blocks, share, FB), BF16)]
    out_specs = [pl.BlockSpec((1, share, FB), lambda f: (jnp.maximum(f - SLOTS, 0), 0, 0))]
    scratch = [pltpu.VMEM((tokens, d), BF16), pltpu.VMEM((d, tokens), BF16), pltpu.VMEM((d, tokens), BF16)]
    scratch += [pltpu.VMEM((tokens, FB), BF16)] * 3
    scratch += [
        pltpu.VMEM((SLOTS, 2, chips, share, FB), BF16),
        pltpu.VMEM((SLOTS, chips, share, FB), BF16),
        pltpu.VMEM((SLOTS, 2, share // 2, FB), BF16),
        pltpu.VMEM((SLOTS, 2, share // 2, FB), BF16),
        pltpu.VMEM((SLOTS, 2, share, FB), BF16),
        pltpu.VMEM((SLOTS, 2, share, FB), BF16),
    ]
    scratch += [pltpu.SemaphoreType.DMA((SLOTS,))] * 2 + [pltpu.SemaphoreType.DMA((SLOTS, 2))] * 4
    if with_input:
        outs.append(jax.ShapeDtypeStruct((tokens, d), BF16))
        out_specs.append(whole)
        scratch.append(pltpu.VMEM((tokens, d), F32))
    return pl.pallas_call(
        functools.partial(backward_kernel, with_input, n),
        grid=(blocks + SLOTS,),
        in_specs=[
            whole,
            whole,
            pl.BlockSpec((1, d, FB), lambda f: (number, 0, jnp.minimum(f, blocks - 1))),
            pl.BlockSpec((1, d, FB), lambda f: (number, 0, jnp.minimum(f, blocks - 1))),
            pl.BlockSpec((1, FB, d), lambda f: (number, jnp.minimum(f, blocks - 1), 0)),
        ],
        out_specs=out_specs,
        out_shape=outs,
        scratch_shapes=scratch,
        compiler_params=pltpu.CompilerParams(
            vmem_limit_bytes=VMEM, dimension_semantics=("arbitrary",), collective_id=number, has_side_effects=True
        ),
        cost_estimate=pl.CostEstimate(
            flops=(16 if with_input else 12) * tokens * d * ff, bytes_accessed=6 * tokens * d + 12 * d * ff, transcendentals=tokens * ff
        ),
        name=f"layer_backward_{number}",
    )(h, g, *weights)


def adamw_kernel(sum_ref, *refs):
    ws, ms, vs, outs = refs[:3], refs[3:6], refs[6:9], refs[-9:]
    share = sum_ref.shape[2] // 3
    some = sum_ref.shape[0]
    for i in range(3):
        if i < 2:
            g = sum_ref[:, 0, i * share : (i + 1) * share, :].reshape(some * share, FB)
        else:
            down = ws[2].shape[1] // some
            pieces = [
                sum_ref[:, 0, 2 * share + j * down : 2 * share + (j + 1) * down, :].reshape(some * down, FB) for j in range(share // down)
            ]
            g = jnp.concatenate(pieces, axis=1)
        g = g.astype(F32)
        w, m, v = ws[i][0].astype(F32), ms[i][0], vs[i][0]
        m = 0.9 * m + 0.1 * g
        v = 0.95 * v + 0.05 * g * g
        step = m * lax.rsqrt(v + 1e-8) + 0.1 * w
        outs[i][0] = (w - 0.02 * step).astype(BF16)
        outs[3 + i][0] = m
        outs[6 + i][0] = v


def adamw(sums, arrays, number, so_far):
    n, blocks, share, _ = sums.shape
    parts = 2
    d, ff = arrays[0].shape[1:]
    wide = pl.BlockSpec((1, d // parts, FB), lambda f, p: (number, p, f))
    tall = pl.BlockSpec((1, FB // parts, d), lambda f, p: (number, f * parts + p, 0))
    three = [wide, wide, tall]
    held = list(so_far) if so_far is not None else []
    return pl.pallas_call(
        adamw_kernel,
        grid=(blocks, parts),
        in_specs=[pl.BlockSpec((n // parts, 1, share, FB), lambda f, p: (p, f, 0, 0))] + three * 3 + [pl.BlockSpec(memory_space=pl.ANY)] * len(held),
        out_specs=three * 3,
        out_shape=[jax.ShapeDtypeStruct(a.shape, a.dtype) for a in arrays],
        input_output_aliases={10 + i: i for i in range(len(held))},
        compiler_params=pltpu.CompilerParams(vmem_limit_bytes=VMEM, dimension_semantics=("arbitrary", "arbitrary")),
        cost_estimate=pl.CostEstimate(flops=3 * 14 * d * ff, bytes_accessed=3 * 22 * d * ff, transcendentals=3 * d * ff),
        name=f"adamw_{number}",
    )(sums, *arrays, *held)


def solution(mesh):
    n = mesh.shape["dp"]

    def step(x, dy, *arrays):
        weights = arrays[:3]
        layers = weights[0].shape[0]
        h, kept = x[0], []
        for number in range(layers):
            kept.append(h)
            if number < layers - 1:
                h = forward(h, weights, number)
        g, sums = dy[0], [None] * layers
        for number in reversed(range(layers)):
            shard, *rest = backward(kept[number], g, weights, number, n, number > 0)
            if number < layers - 1:
                shard, sums[number + 1] = lax.optimization_barrier((shard, sums[number + 1]))
            sums[number] = lax.all_gather(shard, "dp")
            if rest:
                (g,) = rest
        new = None
        for number in reversed(range(layers)):
            new = adamw(sums[number], arrays, number, new)
        return tuple(new)

    return jax.shard_map(
        step,
        mesh=mesh,
        in_specs=(P(("rep", "dp"), None, None),) * 2 + (P(None, None, None),) * 9,
        out_specs=(P("rep", None, None),) * 9,
        check_vma=False,
    )
```

time: 563 us -> 360 us (0.64); the launches traced: 555 us -> 360 us
  Pallas kernels: 0 us -> 333 us
  matrix products: 232 us -> 0 us
  waiting for transfers between devices: 220 us -> 12.4 us
  other arithmetic: 78.3 us -> 0 us
  local copies, waits for them, and re-layouts: 9.94 us -> 0 us
    pallas_call x0 -> x5, Pallas kernels: none -> 333 us  [the longest x2 213 us: backward(): pl.pallas_call(functools.partial(backward_kernel, with_input, n), grid=(b...]
    dot_general x15 -> x0, matrix products: 232 us -> none  [the longest x5 84.2 us: layer(): gate = jnp.dot(a, w['w_gate'], preferred_element_type=jnp.float32)]
    psum x1 -> x0, waiting for transfers between devices: 220 us -> none  [step(): summed[number] = [lax.psum(by_w[name], 'dp') for name in NAMES]]
    convert_element_type x2 -> x0, other arithmetic: 72.4 us -> none  [adamw(): return ((w - 0.02 * step).astype(jnp.bfloat16), m, v)]
    all_gather x0 -> x2, waiting for transfers between devices: none -> 12.3 us  [step(): sums[number] = lax.all_gather(shard, 'dp')]
    unnamed x36 -> x0, local copies, waits for them, and re-layouts: 9.94 us -> none
  transfers between devices with their start and end apart: 1 -> 2, of which waited for: 1 -> 1; matrix products, arithmetic and copies ran while one was open for 0% -> 0% of each run, Pallas kernels for 0% -> 42%
where the time goes in v1:
time: 360 us
  Pallas kernels  333 us (92%)
  between operations  14.1 us (4%)
  waiting for transfers between devices  12.4 us (3%)
    pallas_call x2, Pallas kernels, backward(): pl.pallas_call(functools.partial(backward_kernel, with_input, n), grid=(b...  213 us
    pallas_call x2, Pallas kernels, adamw(): pl.pallas_call(adamw_kernel, grid=(blocks, parts), in_specs=[pl.BlockSpec...  86.8 us
    pallas_call x1, Pallas kernels, forward(): pl.pallas_call(forward_kernel, grid=(ff // FB_FWD,), in_specs=[pl.BlockSp...  33 us
    all_gather x2, waiting for transfers between devices, step(): sums[number] = lax.all_gather(shard, 'dp')  12.3 us
  transfers between devices with their start and end apart: 2, of which 1 were waited for; matrix products, arithmetic and copies ran while one was open for 0% of the time, Pallas kernels for 42%

profile of v1, /device:TPU:112, one launch (start us, length us, event | category | flops | bytes accessed | tf_op | source)
XLA Modules:
  0.0 359.7 jit_solution(13183328398151317736)
XLA Ops:
  7.2 0.1 all-gather.5.cloned.1.call-start
  7.3 33.0 %layer_forward.1.h_ref = bf16[2048,768]{1,0:T(8,128)(2,1)} custom-call(bf16[2048,768]{1,0:T(8,128)(2,1)} %bitcast.7, bf16[2,768,2304]{2,1,0:T(8,128)(2,1)} %refs_0_.3, bf16[2,768,2304]{2,1,0:T(8,128)(2,1)} %refs_1_.3, bf16[2,2304,768]{2,1,0:T(8,128)(2,1)} %refs_2_.3), custom_call_target="tpu_custom_call" | custom-call | flops 21743271936 | bytes 16908288 | tf_op jit(solution)/shard_map/layer_forward/pallas_call | solution.py:77
  40.2 105.5 %layer_backward_1.1 = (bf16[9,288,256]{2,1,0:T(8,128)(2,1)}, bf16[2048,768]{1,0:T(8,128)(2,1)}) custom-call(bf16[2048,768]{1,0:T(8,128)(2,1)} %layer_forward.1.h_ref, bf16[2048,768]{1,0:T(8,128)(2,1)} %bitcast.6, bf16[2,768,2304]{2,1,0:T(8,128)(2,1)} %refs_0_.3, bf16[2,768,2304]{2,1,0:T(8,128)(2,1)} %refs_1_.3, bf16[2,2304,768]{2,1,0:T(8,128)(2,1)} %refs_2_.3), custom_call_target="tpu_custom_call" | custom-call | flops 57982058496 | bytes 30670848 | tf_op jit(solution)/shard_map/layer_backward_1/pallas_call | solution.py:286
  145.8 0.1 all-gather.5.cloned.1.call-update
  145.8 0.2 all-gather.7.cloned.1.call-start
  146.1 107.5 %layer_backward_0.1 = bf16[9,288,256]{2,1,0:T(8,128)(2,1)} custom-call(bf16[2048,768]{1,0:T(8,128)(2,1)} %bitcast.8, bf16[2048,768]{1,0:T(8,128)(2,1)} %get-tuple-element.22.g_ref, bf16[2,768,2304]{2,1,0:T(8,128)(2,1)} %refs_0_.3, bf16[2,768,2304]{2,1,0:T(8,128)(2,1)} %refs_1_.3, bf16[2,2304,768]{2,1,0:T(8,128)(2,1)} %refs_2_.3), custom_call_target="tpu_custom_call" | custom-call | flops 43486543872 | bytes 30670848 | tf_op jit(solution)/shard_map/layer_backward_0/pallas_call | solution.py:286
  253.6 0.0 all-gather.5.cloned.1.call-done
  253.7 0.1 all-gather.7.cloned.1.call-update
  253.7 43.3 %adamw_1.1 = (bf16[2,768,2304]{2,1,0:T(8,128)(2,1)}, bf16[2,768,2304]{2,1,0:T(8,128)(2,1)}, bf16[2,2304,768]{2,1,0:T(8,128)(2,1)}, f32[2,768,2304]{2,1,0:T(8,128...) custom-call(bf16[8,9,288,256]{3,2,1,0:T(8,128)(2,1)} %bitcast.4, ...), custom_call_target="tpu_custom_call" | custom-call | flops 74317824 | bytes 116785152 | tf_op jit(solution)/shard_map/adamw_1/pallas_call | solution.py:340
  297.0 12.3 %all-gather.7.cloned.1.call-done = bf16[72,288,256]{2,1,0:T(8,128)(2,1)} async-done(((bf16[9,288,256]{2,1,0:T(8,128)(2,1)}), bf16[72,288,256]{2,1,0:T(8,128)(2,1)}) %all-gather.7.cloned.1.call-update) | async-done | bytes 10616848 | tf_op jit(solution)/shard_map/all_gather | solution.py:369
  309.3 43.5 %adamw_0.1 = (bf16[2,768,2304]{2,1,0:T(8,128)(2,1)}, bf16[2,768,2304]{2,1,0:T(8,128)(2,1)}, bf16[2,2304,768]{2,1,0:T(8,128)(2,1)}, f32[2,768,2304]{2,1,0:T(8,128...) custom-call(bf16[8,9,288,256]{3,2,1,0:T(8,128)(2,1)} %bitcast.5, ...), custom_call_target="tpu_custom_call", output_to_operand_aliasing={{0}: (10, {}), {1}: (11, {}), {2}: (12, {}), {3}: (13, {}),... | custom-call | flops 74317824 | bytes 116785152 | tf_op jit(solution)/shard_map/adamw_0/pallas_call | solution.py:340
Async XLA Ops:
  7.2 246.5 %all-gather.5.cloned.1.call-start = ((), (), s32[]{:S(2)}) async-start(), calls=%async_computation | async-start | bytes 11943936 | tf_op jit(solution)/shard_map/all_gather | solution.py:369
  145.8 163.4 %all-gather.7.cloned.1.call-start = ((), (), s32[]{:S(2)}) async-start(), calls=%async_computation.1 | async-start | bytes 11943936 | tf_op jit(solution)/shard_map/all_gather | solution.py:369
Sparse Core Ops, SparseCore 0:
  146.0 76.6 all-gather.4
  253.8 55.3 all-gather.6

commit v2 on v1

v2 whole, which is shorter than its diff:
```python
import functools

import jax
import jax.numpy as jnp
from jax import lax
from jax.experimental import pallas as pl
from jax.experimental.pallas import tpu as pltpu
from jax.sharding import PartitionSpec as P

BF16, F32 = jnp.bfloat16, jnp.float32
FB = 256
FB_FWD = 768
TT = 512
VMEM = 60 * 2**20


def dot(a, b):
    return jnp.dot(a, b, preferred_element_type=F32)


def dot_nt(a, b):
    return lax.dot_general(a, b, (((1,), (1,)), ((), ())), preferred_element_type=F32)


def transposed(eye, x):
    return dot_nt(eye, x).astype(BF16)


def scale_of(wide):
    return lax.rsqrt(jnp.mean(wide * wide, -1, keepdims=True) + 1e-6)


def sigmoid(x):
    return 1.0 / (1.0 + jnp.exp(-x))


def forward_kernel(h_ref, wg_ref, wu_ref, wd_ref, out_ref, a_ref, acc_ref):
    step, steps = pl.program_id(0), pl.num_programs(0)
    tokens = h_ref.shape[0]

    @pl.when(step == 0)
    def _():
        def tile(i, _):
            rows = pl.ds(i * TT, TT)
            wide = h_ref[rows, :].astype(F32)
            a_ref[rows, :] = (wide * scale_of(wide)).astype(BF16)
            acc_ref[rows, :] = jnp.zeros((TT, acc_ref.shape[1]), F32)
            return 0

        lax.fori_loop(0, tokens // TT, tile, 0)

    def tile(i, _):
        rows = pl.ds(i * TT, TT)
        a = a_ref[rows, :]
        gate = dot(a, wg_ref[0])
        up = dot(a, wu_ref[0])
        hid = (gate * sigmoid(gate) * up).astype(BF16)
        acc_ref[rows, :] += dot(hid, wd_ref[0])
        return 0

    lax.fori_loop(0, tokens // TT, tile, 0)

    @pl.when(step == steps - 1)
    def _():
        def tile(i, _):
            rows = pl.ds(i * TT, TT)
            down = acc_ref[rows, :].astype(BF16).astype(F32)
            out_ref[rows, :] = (h_ref[rows, :].astype(F32) + down).astype(BF16)
            return 0

        lax.fori_loop(0, tokens // TT, tile, 0)


def forward(h, weights, number):
    tokens, d = h.shape
    ff = weights[0].shape[2]
    return pl.pallas_call(
        forward_kernel,
        grid=(ff // FB_FWD,),
        in_specs=[
            pl.BlockSpec((tokens, d), lambda f: (0, 0), pipeline_mode=pl.Buffered(1)),
            pl.BlockSpec((1, d, FB_FWD), lambda f: (number, 0, f)),
            pl.BlockSpec((1, d, FB_FWD), lambda f: (number, 0, f)),
            pl.BlockSpec((1, FB_FWD, d), lambda f: (number, f, 0)),
        ],
        out_specs=pl.BlockSpec((tokens, d), lambda f: (0, 0), pipeline_mode=pl.Buffered(1)),
        out_shape=jax.ShapeDtypeStruct((tokens, d), BF16),
        scratch_shapes=[pltpu.VMEM((tokens, d), BF16), pltpu.VMEM((tokens, d), F32)],
        compiler_params=pltpu.CompilerParams(vmem_limit_bytes=VMEM, dimension_semantics=("arbitrary",)),
        cost_estimate=pl.CostEstimate(flops=6 * tokens * d * ff, bytes_accessed=4 * tokens * d + 6 * d * ff, transcendentals=tokens * ff),
        name="layer_forward",
    )(h, *weights)


SLOTS, HELD = 4, 6
LATE = 5
MESH = pl.DeviceIdType.MESH


def backward_kernel(n, layers, late, *refs):
    kept, (dy_ref, wg_ref, wu_ref, wd_ref, sums_ref, late_ref), refs = refs[:layers], refs[layers : layers + 6], refs[layers + 6 :]
    g_ref, a_ref, at_ref, gt_ref, hid_ref, dgate_ref, dup_ref, acc_ref, *refs = refs
    own, recv_a, send_b, recv_b, send_c, recv_c, held, *sems = refs
    send_a_sem, recv_a_sem, send_b_sem, recv_b_sem, send_c_sem, recv_c_sem, send_g_sem, recv_g_sem, out_sem = sems
    step = pl.program_id(0)
    tokens, d = dy_ref.shape
    blocks = pl.num_programs(0) - SLOTS - 1
    each, early = blocks // layers, blocks - late
    share, half = own.shape[3], own.shape[3] // 2
    chips = n // 2
    me = lax.axis_index("dp")
    chip, core = lax.div(me, 2), lax.rem(me, 2)
    right_chip, far_chip, left_chip = (lax.rem(chip + i, chips) for i in (1, 2, 3))
    partner = chip * 2 + (1 - core)
    right, far, left = (c * 2 + core for c in (right_chip, far_chip, left_chip))
    sides = (right, left)
    first, second = pl.ds(0, half), pl.ds(half, half)

    def remote(src, dst, send, recv, other):
        return pltpu.make_async_remote_copy(src, dst, send, recv, device_id={"dp": other}, device_id_type=MESH)

    def copy_a(block):
        slot = lax.rem(block, SLOTS)
        return remote(own.at[slot, 1 - core], recv_a.at[slot], send_a_sem.at[slot], recv_a_sem.at[slot], partner)

    def copy_b(block, way):
        slot = lax.rem(block, SLOTS)
        return remote(send_b.at[slot, way], recv_b.at[slot, way], send_b_sem.at[slot, way], recv_b_sem.at[slot, way], sides[way])

    def copy_c(block, way):
        slot = lax.rem(block, SLOTS)
        return remote(send_c.at[slot, way], recv_c.at[slot, way], send_c_sem.at[slot, way], recv_c_sem.at[slot, way], sides[way])

    def copies_g(block, turn):
        slot = lax.rem(block, HELD)
        kind, copies = (
            (0, ((me, None, right), (me, None, left), (me, None, partner))),
            (3, ((left, first, right), (right, second, left), (left, None, partner), (right, None, partner))),
            (7, ((far, None, partner),)),
        )[turn]
        made = []
        for i, (shard, rows, other) in enumerate(copies, kind):
            place = held.at[slot, shard] if rows is None else held.at[slot, shard, rows]
            made.append(remote(place, place, send_g_sem.at[i, slot], recv_g_sem.at[i, slot], other))
        return made

    def copy_out(block):
        slot = lax.rem(block, HELD)
        return pltpu.make_async_copy(held.at[slot], sums_ref.at[:, block], out_sem.at[slot])

    def copy_late(block):
        slot = lax.rem(block, HELD)
        return pltpu.make_async_copy(held.at[slot, me], late_ref.at[block - early], out_sem.at[slot])

    def on_chip(slot, which, rows):
        return own[slot, core, which, rows].astype(F32) + recv_a[slot, which, rows].astype(F32)

    def stage(after, low, high):
        def run(do):
            @pl.when((step >= after + low) & (step < after + high))
            def _():
                do(step - after)

        return run

    @pl.when(step == 0)
    def _():
        barrier = pltpu.get_barrier_semaphore()
        for other in (partner, *sides):
            pl.semaphore_signal(barrier, inc=1, device_id={"dp": other}, device_id_type=MESH)

    @pl.when(step == 1)
    def _():
        pl.semaphore_wait(pltpu.get_barrier_semaphore(), 3)

    @stage(8, 0, early)
    def _(block):
        copy_out(block).wait()

    @stage(7, 0, early)
    def _(block):
        for copy in copies_g(block, 2):
            copy.wait()
        copy_out(block).start()

    @stage(6, 0, early)
    def _(block):
        for copy in copies_g(block, 1):
            copy.wait()
        for copy in copies_g(block, 2):
            copy.start()

    @stage(5, 0, early)
    def _(block):
        for copy in copies_g(block, 0):
            copy.wait()
        for copy in copies_g(block, 1):
            copy.start()

    @stage(5, early, blocks)
    def _(block):
        copy_late(block).wait()

    @stage(4, 0, blocks)
    def _(block):
        slot = lax.rem(block, SLOTS)
        copy_c(block, 0).wait()
        copy_c(block, 1).wait()
        for rows in (first, second):
            total = on_chip(slot, chip, rows) + recv_c[slot, 0, rows].astype(F32) + recv_c[slot, 1, rows].astype(F32)
            held[lax.rem(block, HELD), me, rows] = total.astype(BF16)

    @stage(3, 0, blocks)
    def _(block):
        slot = lax.rem(block, SLOTS)
        copy_b(block, 0).wait()
        copy_b(block, 1).wait()
        send_c[slot, 0, first] = (on_chip(slot, right_chip, first) + recv_b[slot, 0].astype(F32)).astype(BF16)
        send_c[slot, 0, second] = on_chip(slot, right_chip, second).astype(BF16)
        send_c[slot, 1, first] = on_chip(slot, left_chip, first).astype(BF16)
        send_c[slot, 1, second] = (on_chip(slot, left_chip, second) + recv_b[slot, 1].astype(F32)).astype(BF16)
        copy_c(block, 0).start()
        copy_c(block, 1).start()

    @stage(2, 0, blocks)
    def _(block):
        slot = lax.rem(block, SLOTS)
        copy_a(block).wait()
        send_b[slot, 0] = on_chip(slot, far_chip, first).astype(BF16)
        send_b[slot, 1] = on_chip(slot, far_chip, second).astype(BF16)
        copy_b(block, 0).start()
        copy_b(block, 1).start()

    @stage(1, 0, blocks)
    def _(block):
        copy_a(block).start()

    @stage(4, 0, early)
    def _(block):
        for copy in copies_g(block, 0):
            copy.start()

    @stage(4, early, blocks)
    def _(block):
        copy_late(block).start()

    eye = (lax.broadcasted_iota(jnp.int32, (FB, FB), 0) == lax.broadcasted_iota(jnp.int32, (FB, FB), 1)).astype(BF16)

    for number in range(layers):

        @pl.when(step == (layers - 1 - number) * each)
        def _(number=number):
            def tile(i, _):
                rows = pl.ds(pl.multiple_of(i * TT, TT), TT)
                if number == layers - 1:
                    g_ref[rows, :] = dy_ref[rows, :]
                else:
                    wide = kept[number + 1][rows, :].astype(F32)
                    scale = scale_of(wide)
                    da = acc_ref[rows, :].astype(BF16).astype(F32)
                    along = jnp.mean(da * wide, -1, keepdims=True)
                    dwide = (da * scale - wide * (scale * scale * scale * along)).astype(BF16)
                    g_ref[rows, :] = (g_ref[rows, :].astype(F32) + dwide.astype(F32)).astype(BF16)
                if number:
                    acc_ref[rows, :] = jnp.zeros((TT, d), F32)
                wide = kept[number][rows, :].astype(F32)
                a_ref[rows, :] = (wide * scale_of(wide)).astype(BF16)
                for j in range(d // FB):
                    at_ref[j * FB : (j + 1) * FB, rows] = transposed(eye, a_ref[rows, j * FB : (j + 1) * FB])
                    gt_ref[j * FB : (j + 1) * FB, rows] = transposed(eye, g_ref[rows, j * FB : (j + 1) * FB])
                return 0

            lax.fori_loop(0, tokens // TT, tile, 0)

    @stage(0, 0, blocks)
    def _(block):
        slot = lax.rem(block, SLOTS)
        wg, wu, wd = wg_ref[0], wu_ref[0], wd_ref[0]
        for i in range(tokens // TT):
            rows = pl.ds(i * TT, TT)
            a = a_ref[rows, :]
            gate, up = dot(a, wg), dot(a, wu)
            dhid = dot_nt(g_ref[rows, :], wd).astype(BF16).astype(F32)
            sig = sigmoid(gate)
            silu = gate * sig
            hid_ref[rows, :] = (silu * up).astype(BF16)
            dup_ref[rows, :] = (dhid * silu).astype(BF16)
            dgate_ref[rows, :] = (dhid * up * (sig + silu * (1.0 - sig))).astype(BF16)
        part, down = d // n, FB // n
        for i in range(d // FB):
            rows = pl.ds(i * FB, FB)
            dwg = dot(at_ref[rows, :], dgate_ref[...]).astype(BF16)
            dwu = dot(at_ref[rows, :], dup_ref[...]).astype(BF16)
            dwd = transposed(eye, dot(gt_ref[rows, :], hid_ref[...]).astype(BF16))
            lo, hi = i * FB, (i + 1) * FB
            for k in range(n):
                top, end = max(lo, k * part), min(hi, (k + 1) * part)
                if top < end:
                    own[slot, k % 2, k // 2, top - k * part : end - k * part, :] = dwg[top - lo : end - lo]
                    own[slot, k % 2, k // 2, part + top - k * part : part + end - k * part, :] = dwu[top - lo : end - lo]
                own[slot, k % 2, k // 2, 2 * part + i * down : 2 * part + (i + 1) * down, :] = dwd[k * down : (k + 1) * down]

    @stage(0, 0, blocks - each)
    def _(block):
        for i in range(tokens // TT):
            rows = pl.ds(i * TT, TT)
            acc_ref[rows, :] += dot_nt(dgate_ref[rows, :], wg_ref[0]) + dot_nt(dup_ref[rows, :], wu_ref[0])


def backward(kept, dy, weights, n, late):
    tokens, d = dy.shape
    layers, _, ff = weights[0].shape
    each = ff // FB
    blocks = layers * each
    chips, share = n // 2, 3 * d // n
    assert chips == 4 and 3 < late <= each
    whole = pl.BlockSpec((tokens, d), lambda s: (0, 0), pipeline_mode=pl.Buffered(1))

    def at(s):
        s = jnp.minimum(s, blocks - 1)
        return layers - 1 - lax.div(s, each), lax.rem(s, each)

    def wide_at(s):
        number, f = at(s)
        return number, 0, f

    def tall_at(s):
        number, f = at(s)
        return number, f, 0

    def vmem(*shape):
        return pltpu.VMEM(shape, BF16)

    scratch = [vmem(tokens, d), vmem(tokens, d), vmem(d, tokens), vmem(d, tokens)]
    scratch += [vmem(tokens, FB)] * 3 + [pltpu.VMEM((tokens, d), F32)]
    scratch += [vmem(SLOTS, 2, chips, share, FB), vmem(SLOTS, chips, share, FB)]
    scratch += [vmem(SLOTS, 2, share // 2, FB)] * 2 + [vmem(SLOTS, 2, share, FB)] * 2 + [vmem(HELD, n, share, FB)]
    scratch += [pltpu.SemaphoreType.DMA((SLOTS,))] * 2 + [pltpu.SemaphoreType.DMA((SLOTS, 2))] * 4
    scratch += [pltpu.SemaphoreType.DMA((8, HELD))] * 2 + [pltpu.SemaphoreType.DMA((HELD,))]
    return pl.pallas_call(
        functools.partial(backward_kernel, n, layers, late),
        grid=(blocks + SLOTS + 1,),
        in_specs=[whole] * (layers + 1)
        + [pl.BlockSpec((1, d, FB), wide_at), pl.BlockSpec((1, d, FB), wide_at), pl.BlockSpec((1, FB, d), tall_at)],
        out_specs=[pl.BlockSpec(memory_space=pl.ANY)] * 2,
        out_shape=[
            jax.ShapeDtypeStruct((n, blocks - late, share, FB), BF16),
            jax.ShapeDtypeStruct((late, share, FB), BF16),
        ],
        scratch_shapes=scratch,
        compiler_params=pltpu.CompilerParams(
            vmem_limit_bytes=VMEM, dimension_semantics=("arbitrary",), collective_id=0, has_side_effects=True
        ),
        cost_estimate=pl.CostEstimate(
            flops=(16 * layers - 4) * tokens * d * ff, bytes_accessed=6 * tokens * d + 12 * layers * d * ff, transcendentals=layers * tokens * ff
        ),
        name="backward",
    )(*kept, dy, *weights)


def adamw_kernel(sum_ref, *refs):
    ws, ms, vs, outs = refs[:3], refs[3:6], refs[6:9], refs[-9:]
    share = sum_ref.shape[2] // 3
    some = sum_ref.shape[0]
    for i in range(3):
        if i < 2:
            g = sum_ref[:, 0, i * share : (i + 1) * share, :].reshape(some * share, FB)
        else:
            down = ws[2].shape[1] // some
            pieces = [
                sum_ref[:, 0, 2 * share + j * down : 2 * share + (j + 1) * down, :].reshape(some * down, FB) for j in range(share // down)
            ]
            g = jnp.concatenate(pieces, axis=1)
        g = g.astype(F32)
        w, m, v = ws[i][0].astype(F32), ms[i][0], vs[i][0]
        m = 0.9 * m + 0.1 * g
        v = 0.95 * v + 0.05 * g * g
        step = m * lax.rsqrt(v + 1e-8) + 0.1 * w
        outs[i][0] = (w - 0.02 * step).astype(BF16)
        outs[3 + i][0] = m
        outs[6 + i][0] = v


def adamw(sums, arrays, number, blocks, offset, so_far):
    n, _, share, _ = sums.shape
    d = arrays[0].shape[1]
    parts = 2
    low, high = blocks
    wide = pl.BlockSpec((1, d // parts, FB), lambda f, p: (number, p, low + f))
    tall = pl.BlockSpec((1, FB // parts, d), lambda f, p: (number, (low + f) * parts + p, 0))
    three = [wide, wide, tall]
    held = list(so_far) if so_far is not None else []
    size = 3 * d * FB * (high - low)
    return pl.pallas_call(
        adamw_kernel,
        grid=(high - low, parts),
        in_specs=[pl.BlockSpec((n // parts, 1, share, FB), lambda f, p: (p, offset + f, 0, 0))]
        + three * 3
        + [pl.BlockSpec(memory_space=pl.ANY)] * len(held),
        out_specs=three * 3,
        out_shape=[jax.ShapeDtypeStruct(a.shape, a.dtype) for a in arrays],
        input_output_aliases={10 + i: i for i in range(len(held))},
        compiler_params=pltpu.CompilerParams(vmem_limit_bytes=VMEM, dimension_semantics=("arbitrary", "arbitrary")),
        cost_estimate=pl.CostEstimate(flops=14 * size, bytes_accessed=22 * size, transcendentals=size),
        name=f"adamw_{number}_{low}",
    )(sums, *arrays, *held)


def solution(mesh):
    n = mesh.shape["dp"]

    def step(x, dy, *arrays):
        weights = arrays[:3]
        layers, _, ff = weights[0].shape
        each = ff // FB
        kept = [x[0]]
        for number in range(layers - 1):
            kept.append(forward(kept[-1], weights, number))
        sums, shards = backward(kept, dy[0], weights, n, LATE)
        late = lax.all_gather(shards, "dp")
        new = None
        for number in reversed(range(layers)):
            high = each if number else each - LATE
            if high:
                new = adamw(sums, arrays, number, (0, high), (layers - 1 - number) * each, new)
        return tuple(adamw(late, arrays, 0, (each - LATE, each), 0, new))

    return jax.shard_map(
        step,
        mesh=mesh,
        in_specs=(P(("rep", "dp"), None, None),) * 2 + (P(None, None, None),) * 9,
        out_specs=(P("rep", None, None),) * 9,
        check_vma=False,
    )
```

time: 360 us -> 348 us (0.967)
  waiting for transfers between devices: 12.4 us -> 0.08 us
    all_gather x2 -> x1, waiting for transfers between devices: 12.3 us -> 0.02 us  [step(): late = lax.all_gather(shards, 'dp')]
  transfers between devices with their start and end apart: 2 -> 1, of which waited for: 1 -> 0; matrix products, arithmetic and copies ran while one was open for 0% -> 0% of each run, Pallas kernels for 42% -> 18%
where the time goes in v2:
time: 348 us
  Pallas kernels  334 us (96%)
  between operations  14.1 us (4%)
    pallas_call x1, Pallas kernels, backward(): pl.pallas_call(functools.partial(backward_kernel, n, layers, late), grid=...  214 us
    pallas_call x3, Pallas kernels, adamw(): pl.pallas_call(adamw_kernel, grid=(high - low, parts), in_specs=[pl.Block...  87.3 us
    pallas_call x1, Pallas kernels, forward(): pl.pallas_call(forward_kernel, grid=(ff // FB_FWD,), in_specs=[pl.BlockSp...  33 us
  transfers between devices with their start and end apart: 1, of which 0 were waited for; matrix products, arithmetic and copies ran while one was open for 0% of the time, Pallas kernels for 18%

profile of v2, /device:TPU:112, one launch (start us, length us, event | category | flops | bytes accessed | tf_op | source)
XLA Modules:
  0.0 348.4 jit_solution(14606631752741672927)
XLA Ops:
  7.2 0.1 all-gather.3.cloned.1.call-start
  7.3 33.0 %layer_forward.1.refs_1_ = bf16[2048,768]{1,0:T(8,128)(2,1)} custom-call(bf16[2048,768]{1,0:T(8,128)(2,1)} %bitcast.4, bf16[2,768,2304]{2,1,0:T(8,128)(2,1)} %refs_0_.5, bf16[2,768,2304]{2,1,0:T(8,128)(2,1)} %refs_1_.5, bf16[2,2304,768]{2,1,0:T(8,128)(2,1)} %refs_2_.5), custom_call_target="tpu_custom_call" | custom-call | flops 21743271936 | bytes 16908288 | tf_op jit(solution)/shard_map/layer_forward/pallas_call | solution.py:77
  40.2 213.8 %backward.1 = (bf16[8,13,288,256]{3,2,1,0:T(8,128)(2,1)}, bf16[5,288,256]{2,1,0:T(8,128)(2,1)}) custom-call(bf16[2048,768]{1,0:T(8,128)(2,1)} %bitcast.5, bf16[2048,768]{1,0:T(8,128)(2,1)} %layer_forward.1.refs_1_, bf16[2048,768]{1,0:T(8,128)(2,1)} %bitcast.6, bf16[2,768,2304]{2,1,0:T(8,128)(2,1)} %refs_0_.5, bf16[2,768,2304]{2,1,0:T(8,128)(2,1)} %refs_1_.5, ...), custom_call_target="tpu_custom_call" | custom-call | flops 101468602368 | bytes 51904512 | tf_op jit(solution)/shard_map/backward/pallas_call | solution.py:340
  254.0 0.1 all-gather.3.cloned.1.call-update
  254.1 43.3 %adamw_1_0.1 = (bf16[2,768,2304]{2,1,0:T(8,128)(2,1)}, bf16[2,768,2304]{2,1,0:T(8,128)(2,1)}, bf16[2,2304,768]{2,1,0:T(8,128)(2,1)}, f32[2,768,2304]{2,1,0:T(8,1...) custom-call(bf16[8,13,288,256]{3,2,1,0:T(8,128)(2,1)} %get-tuple-ele, ...), custom_call_target="tpu_custom_call" | custom-call | flops 74317824 | bytes 116785152 | tf_op jit(solution)/shard_map/adamw_1_0/pallas_call | solution.py:394
  297.4 19.7 %adamw_0_0.1 = (bf16[2,768,2304]{2,1,0:T(8,128)(2,1)}, bf16[2,768,2304]{2,1,0:T(8,128)(2,1)}, bf16[2,2304,768]{2,1,0:T(8,128)(2,1)}, f32[2,768,2304]{2,1,0:T(8,1...) custom-call(bf16[8,13,288,256]{3,2,1,0:T(8,128)(2,1)} %get-tuple-ele, ...), custom_call_target="tpu_custom_call", output_to_operand_aliasing={{0}: (10, {}), {1}: (11, {}), {2}: (12, {}), {3}: (13, {}),... | custom-call | flops 33030144 | bytes 51904512 | tf_op jit(solution)/shard_map/adamw_0_0/pallas_call | solution.py:394
  317.0 0.0 all-gather.3.cloned.1.call-done
  317.1 24.4 %adamw_0_4.1 = (bf16[2,768,2304]{2,1,0:T(8,128)(2,1)}, bf16[2,768,2304]{2,1,0:T(8,128)(2,1)}, bf16[2,2304,768]{2,1,0:T(8,128)(2,1)}, f32[2,768,2304]{2,1,0:T(8,1...) custom-call(bf16[8,5,288,256]{3,2,1,0:T(8,128)(2,1)} %bitcast.3, ...), custom_call_target="tpu_custom_call", output_to_operand_aliasing={{0}: (10, {}), {1}: (11, {}), {2}: (12, {}), {3}: (13, {}),... | custom-call | flops 41287680 | bytes 64880640 | tf_op jit(solution)/shard_map/adamw_0_4/pallas_call | solution.py:394
Async XLA Ops:
  7.2 309.9 %all-gather.3.cloned.1.call-start = ((), (), s32[]{:S(2)}) async-start(), calls=%async_computation | async-start | bytes 6635520 | tf_op jit(solution)/shard_map/all_gather | solution.py:420
Sparse Core Ops, SparseCore 0:
  254.2 35.2 all-gather.2

commit v3 on v2

--- a/solution.py
+++ b/solution.py
@@ -9,8 +9,8 @@
 
 BF16, F32 = jnp.bfloat16, jnp.float32
 FB = 256
-FB_FWD = 768
-TT = 512
+FB_FWD = 256
+TT, TT_FWD = 512, 1024
 VMEM = 60 * 2**20
 
 
@@ -34,66 +34,36 @@
     return 1.0 / (1.0 + jnp.exp(-x))
 
 
-def forward_kernel(h_ref, wg_ref, wu_ref, wd_ref, out_ref, a_ref, acc_ref):
-    step, steps = pl.program_id(0), pl.num_programs(0)
-    tokens = h_ref.shape[0]
-
-    @pl.when(step == 0)
-    def _():
-        def tile(i, _):
-            rows = pl.ds(i * TT, TT)
-            wide = h_ref[rows, :].astype(F32)
-            a_ref[rows, :] = (wide * scale_of(wide)).astype(BF16)
-            acc_ref[rows, :] = jnp.zeros((TT, acc_ref.shape[1]), F32)
-            return 0
-
-        lax.fori_loop(0, tokens // TT, tile, 0)
-
-    def tile(i, _):
-        rows = pl.ds(i * TT, TT)
-        a = a_ref[rows, :]
-        gate = dot(a, wg_ref[0])
-        up = dot(a, wu_ref[0])
-        hid = (gate * sigmoid(gate) * up).astype(BF16)
-        acc_ref[rows, :] += dot(hid, wd_ref[0])
-        return 0
-
-    lax.fori_loop(0, tokens // TT, tile, 0)
-
-    @pl.when(step == steps - 1)
-    def _():
-        def tile(i, _):
-            rows = pl.ds(i * TT, TT)
-            down = acc_ref[rows, :].astype(BF16).astype(F32)
-            out_ref[rows, :] = (h_ref[rows, :].astype(F32) + down).astype(BF16)
-            return 0
-
-        lax.fori_loop(0, tokens // TT, tile, 0)
+def forward_kernel(h_ref, wg_ref, wu_ref, wd_ref, out_ref, hid_ref):
+    wide = h_ref[...].astype(F32)
+    a = (wide * scale_of(wide)).astype(BF16)
+    for f in range(0, hid_ref.shape[1], FB_FWD):
+        units = pl.ds(f, FB_FWD)
+        gate, up = dot(a, wg_ref[0, :, units]), dot(a, wu_ref[0, :, units])
+        hid_ref[:, units] = (gate * sigmoid(gate) * up).astype(BF16)
+    down = dot(hid_ref[...], wd_ref[0]).astype(BF16).astype(F32)
+    out_ref[...] = (h_ref[...].astype(F32) + down).astype(BF16)
 
 
 def forward(h, weights, number):
     tokens, d = h.shape
     ff = weights[0].shape[2]
+    tile = pl.BlockSpec((TT_FWD, d), lambda t: (t, 0))
     return pl.pallas_call(
         forward_kernel,
-        grid=(ff // FB_FWD,),
-        in_specs=[
-            pl.BlockSpec((tokens, d), lambda f: (0, 0), pipeline_mode=pl.Buffered(1)),
-            pl.BlockSpec((1, d, FB_FWD), lambda f: (number, 0, f)),
-            pl.BlockSpec((1, d, FB_FWD), lambda f: (number, 0, f)),
-            pl.BlockSpec((1, FB_FWD, d), lambda f: (number, f, 0)),
-        ],
-        out_specs=pl.BlockSpec((tokens, d), lambda f: (0, 0), pipeline_mode=pl.Buffered(1)),
+        grid=(tokens // TT_FWD,),
+        in_specs=[tile] + [pl.BlockSpec((1, *w.shape[1:]), lambda t: (number, 0, 0), pipeline_mode=pl.Buffered(1)) for w in weights],
+        out_specs=tile,
         out_shape=jax.ShapeDtypeStruct((tokens, d), BF16),
-        scratch_shapes=[pltpu.VMEM((tokens, d), BF16), pltpu.VMEM((tokens, d), F32)],
+        scratch_shapes=[pltpu.VMEM((TT_FWD, ff), BF16)],
         compiler_params=pltpu.CompilerParams(vmem_limit_bytes=VMEM, dimension_semantics=("arbitrary",)),
         cost_estimate=pl.CostEstimate(flops=6 * tokens * d * ff, bytes_accessed=4 * tokens * d + 6 * d * ff, transcendentals=tokens * ff),
         name="layer_forward",
     )(h, *weights)
 
 
-SLOTS, HELD = 4, 6
-LATE = 5
+SLOTS, HELD = 4, 8
+LATE = 7
 MESH = pl.DeviceIdType.MESH
 
 
@@ -173,29 +143,15 @@
     def _():
         pl.semaphore_wait(pltpu.get_barrier_semaphore(), 3)
 
-    @stage(8, 0, early)
+    @stage(10, 0, early)
     def _(block):
         copy_out(block).wait()
 
-    @stage(7, 0, early)
+    @stage(9, 0, early)
     def _(block):
         for copy in copies_g(block, 2):
             copy.wait()
         copy_out(block).start()
-
-    @stage(6, 0, early)
-    def _(block):
-        for copy in copies_g(block, 1):
-            copy.wait()
-        for copy in copies_g(block, 2):
-            copy.start()
-
-    @stage(5, 0, early)
-    def _(block):
-        for copy in copies_g(block, 0):
-            copy.wait()
-        for copy in copies_g(block, 1):
-            copy.start()
 
     @stage(5, early, blocks)
     def _(block):
@@ -234,6 +190,20 @@
     @stage(1, 0, blocks)
     def _(block):
         copy_a(block).start()
+
+    @stage(8, 0, early)
+    def _(block):
+        for copy in copies_g(block, 1):
+            copy.wait()
+        for copy in copies_g(block, 2):
+            copy.start()
+
+    @stage(6, 0, early)
+    def _(block):
+        for copy in copies_g(block, 0):
+            copy.wait()
+        for copy in copies_g(block, 1):
+            copy.start()
 
     @stage(4, 0, early)
     def _(block):
@@ -289,9 +259,10 @@
         part, down = d // n, FB // n
         for i in range(d // FB):
             rows = pl.ds(i * FB, FB)
+            dwd = dot(gt_ref[rows, :], hid_ref[...]).astype(BF16)
             dwg = dot(at_ref[rows, :], dgate_ref[...]).astype(BF16)
             dwu = dot(at_ref[rows, :], dup_ref[...]).astype(BF16)
-            dwd = transposed(eye, dot(gt_ref[rows, :], hid_ref[...]).astype(BF16))
+            dwd = dwd.T
             lo, hi = i * FB, (i + 1) * FB
             for k in range(n):
                 top, end = max(lo, k * part), min(hi, (k + 1) * part)
@@ -313,7 +284,7 @@
     each = ff // FB
     blocks = layers * each
     chips, share = n // 2, 3 * d // n
-    assert chips == 4 and 3 < late <= each
+    assert chips == 4 and 5 < late <= each
     whole = pl.BlockSpec((tokens, d), lambda s: (0, 0), pipeline_mode=pl.Buffered(1))
 
     def at(s):
@@ -381,28 +352,36 @@
         outs[6 + i][0] = v
 
 
-def adamw(sums, arrays, number, blocks, offset, so_far):
+def adamw(sums, arrays, first, last, so_far):
     n, _, share, _ = sums.shape
-    d = arrays[0].shape[1]
-    parts = 2
-    low, high = blocks
-    wide = pl.BlockSpec((1, d // parts, FB), lambda f, p: (number, p, low + f))
-    tall = pl.BlockSpec((1, FB // parts, d), lambda f, p: (number, (low + f) * parts + p, 0))
+    layers, d, ff = arrays[0].shape
+    each = ff // FB
+
+    def at(f):
+        return layers - 1 - lax.div(first + f, each), lax.rem(first + f, each)
+
+    def wide_at(f):
+        number, block = at(f)
+        return number, 0, block
+
+    def tall_at(f):
+        number, block = at(f)
+        return number, block, 0
+
+    wide, tall = pl.BlockSpec((1, d, FB), wide_at), pl.BlockSpec((1, FB, d), tall_at)
     three = [wide, wide, tall]
     held = list(so_far) if so_far is not None else []
-    size = 3 * d * FB * (high - low)
+    size = 3 * d * FB * (last - first)
     return pl.pallas_call(
         adamw_kernel,
-        grid=(high - low, parts),
-        in_specs=[pl.BlockSpec((n // parts, 1, share, FB), lambda f, p: (p, offset + f, 0, 0))]
-        + three * 3
-        + [pl.BlockSpec(memory_space=pl.ANY)] * len(held),
+        grid=(last - first,),
+        in_specs=[pl.BlockSpec((n, 1, share, FB), lambda f: (0, f, 0, 0))] + three * 3 + [pl.BlockSpec(memory_space=pl.ANY)] * len(held),
         out_specs=three * 3,
         out_shape=[jax.ShapeDtypeStruct(a.shape, a.dtype) for a in arrays],
         input_output_aliases={10 + i: i for i in range(len(held))},
-        compiler_params=pltpu.CompilerParams(vmem_limit_bytes=VMEM, dimension_semantics=("arbitrary", "arbitrary")),
+        compiler_params=pltpu.CompilerParams(vmem_limit_bytes=VMEM, dimension_semantics=("arbitrary",)),
         cost_estimate=pl.CostEstimate(flops=14 * size, bytes_accessed=22 * size, transcendentals=size),
-        name=f"adamw_{number}_{low}",
+        name=f"adamw_{first}",
     )(sums, *arrays, *held)
 
 
@@ -412,18 +391,14 @@
     def step(x, dy, *arrays):
         weights = arrays[:3]
         layers, _, ff = weights[0].shape
-        each = ff // FB
         kept = [x[0]]
         for number in range(layers - 1):
             kept.append(forward(kept[-1], weights, number))
         sums, shards = backward(kept, dy[0], weights, n, LATE)
         late = lax.all_gather(shards, "dp")
-        new = None
-        for number in reversed(range(layers)):
-            high = each if number else each - LATE
-            if high:
-                new = adamw(sums, arrays, number, (0, high), (layers - 1 - number) * each, new)
-        return tuple(adamw(late, arrays, 0, (each - LATE, each), 0, new))
+        blocks = layers * (ff // FB)
+        new = adamw(sums, arrays, 0, blocks - LATE, None)
+        return tuple(adamw(late, arrays, blocks - LATE, blocks, new))
 
     return jax.shard_map(
         step,

time: 348 us -> 308 us (0.89)
  Pallas kernels: 334 us -> 293 us
    pallas_call x1, Pallas kernels: 214 us -> 182 us  [backward(): pl.pallas_call(functools.partial(backward_kernel, n, layers, late), grid=...]
    pallas_call x4 -> x3, Pallas kernels: 120 us -> 111 us  [the longest x2 82.1 us: adamw(): pl.pallas_call(adamw_kernel, grid=(last - first,), in_specs=[pl.BlockSpec...]
  transfers between devices with their start and end apart: 1 -> 1, of which waited for: 0 -> 0; matrix products, arithmetic and copies ran while one was open for 0% -> 0% of each run, Pallas kernels for 18% -> 16%
where the time goes in v3:
time: 308 us; the launch traced here: 307 us
  Pallas kernels  293 us (95%)
  between operations  14.1 us (5%)
    pallas_call x1, Pallas kernels, backward(): pl.pallas_call(functools.partial(backward_kernel, n, layers, late), grid=...  182 us
    pallas_call x2, Pallas kernels, adamw(): pl.pallas_call(adamw_kernel, grid=(last - first,), in_specs=[pl.BlockSpec...  82.1 us
    pallas_call x1, Pallas kernels, forward(): pl.pallas_call(forward_kernel, grid=(tokens // TT_FWD,), in_specs=[tile]...  28.8 us
  transfers between devices with their start and end apart: 1, of which 0 were waited for; matrix products, arithmetic and copies ran while one was open for 0% of the time, Pallas kernels for 16%

profile of v3, /device:TPU:112, one launch (start us, length us, event | category | flops | bytes accessed | tf_op | source)
XLA Modules:
  0.0 307.5 jit_solution(18090757308831030216)
XLA Ops:
  7.2 0.1 all-gather.3.cloned.1.call-start
  7.3 28.8 %layer_forward.1.refs_1_ = bf16[2048,768]{1,0:T(8,128)(2,1)} custom-call(bf16[2048,768]{1,0:T(8,128)(2,1)} %bitcast.4, bf16[2,768,2304]{2,1,0:T(8,128)(2,1)} %refs_0_.3, bf16[2,768,2304]{2,1,0:T(8,128)(2,1)} %refs_1_.3, bf16[2,2304,768]{2,1,0:T(8,128)(2,1)} %refs_2_.3), custom_call_target="tpu_custom_call" | custom-call | flops 21743271936 | bytes 16908288 | tf_op jit(solution)/shard_map/layer_forward/pallas_call | solution.py:52
  36.0 182.3 %backward.1 = (bf16[8,11,288,256]{3,2,1,0:T(8,128)(2,1)}, bf16[7,288,256]{2,1,0:T(8,128)(2,1)}) custom-call(bf16[2048,768]{1,0:T(8,128)(2,1)} %bitcast.5, bf16[2048,768]{1,0:T(8,128)(2,1)} %layer_forward.1.refs_1_, bf16[2048,768]{1,0:T(8,128)(2,1)} %bitcast.6, bf16[2,768,2304]{2,1,0:T(8,128)(2,1)} %refs_0_.3, bf16[2,768,2304]{2,1,0:T(8,128)(2,1)} %refs_1_.3, ...), custom_call_target="tpu_custom_call" | custom-call | flops 101468602368 | bytes 51904512 | tf_op jit(solution)/shard_map/backward/pallas_call | solution.py:311
  218.4 0.1 all-gather.3.cloned.1.call-update
  218.4 49.5 %adamw_0.1 = (bf16[2,768,2304]{2,1,0:T(8,128)(2,1)}, bf16[2,768,2304]{2,1,0:T(8,128)(2,1)}, bf16[2,2304,768]{2,1,0:T(8,128)(2,1)}, f32[2,768,2304]{2,1,0:T(8,128...) custom-call(bf16[8,11,288,256]{3,2,1,0:T(8,128)(2,1)} %get-tuple-ele, ...), custom_call_target="tpu_custom_call" | custom-call | flops 90832896 | bytes 142737408 | tf_op jit(solution)/shard_map/adamw_0/pallas_call | solution.py:375
  268.0 0.0 all-gather.3.cloned.1.call-done
  268.0 32.6 %adamw_11.1 = (bf16[2,768,2304]{2,1,0:T(8,128)(2,1)}, bf16[2,768,2304]{2,1,0:T(8,128)(2,1)}, bf16[2,2304,768]{2,1,0:T(8,128)(2,1)}, f32[2,768,2304]{2,1,0:T(8,12...) custom-call(bf16[8,7,288,256]{3,2,1,0:T(8,128)(2,1)} %bitcast.3, ...), custom_call_target="tpu_custom_call", output_to_operand_aliasing={{0}: (10, {}), {1}: (11, {}), {2}: (12, {}), {3}: (13, {}),... | custom-call | flops 57802752 | bytes 90832896 | tf_op jit(solution)/shard_map/adamw_11/pallas_call | solution.py:375
Async XLA Ops:
  7.2 260.8 %all-gather.3.cloned.1.call-start = ((), (), s32[]{:S(2)}) async-start(), calls=%async_computation | async-start | bytes 9289728 | tf_op jit(solution)/shard_map/all_gather | solution.py:398
Sparse Core Ops, SparseCore 0:
  218.5 45.1 all-gather.2
